TPU v7x, 32 devices: a whole 2x2x4 slice. The times are simulated.
32 devices in a mesh: rep: 2 (over y), span: 2 (over core), seq: 4 (over z), tp: 2 (over x).
Axes of the slice: x: 2, y: 2, z: 4, core: 2. Of those that a mesh axis runs over, the one named last changes fastest.
Arguments:
- queries: bfloat16 [8, 512, 24, 128], P(('rep', 'span'), 'seq', 'tp'), parts along dimension 0, may hold values from -110 to 110
- key_states: bfloat16 [8, 512, 4, 128], P(('rep', 'span'), 'seq', 'tp'), parts along dimension 0, may hold values from -11 to 11
- value_states: bfloat16 [8, 512, 4, 128], P(('rep', 'span'), 'seq', 'tp'), parts along dimension 0, may hold values from -6 to 6
- out_weight: bfloat16 [3072, 6144], P('tp', 'seq'), may hold values from -0.109375 to 0.109375
- noise_table: float32 [64, 6144], P(None, 'tp'), may hold values from 0.5 to 2
- plan: int32 [8], P('rep'), parts along dimension 0, may hold values from 0 to 63
Outputs:
- branch_out: bfloat16 [8, 512, 6144], P(('rep', 'span'), 'seq', 'tp'), parts along dimension 0
There are 2 independent parts, one for each index of `rep`. A program takes and returns all parts, laid end to end along the dimension named above; an argument that names none is the same for every part. Nothing has to cross between parts.
All inputs are finite; a program needn't handle non-finite values.
Results may differ from a plain program's by a relative error of at most 0.014.
Values may be sent and summed in bfloat16 or wider, within the bound.
A program may use at most 128 MiB of HBM per device.

v0:
```python
import jax
import jax.numpy as jnp
from jax import lax
from jax.sharding import PartitionSpec as P


def fold_block(carried, query_rows, key_rows, value_rows, factor):
    maxima, totals, weighted = carried
    scores = (
        jnp.einsum("tkgd,skd->tkgs", query_rows, key_rows, preferred_element_type=jnp.float32)
        * factor
    )
    highest = jnp.maximum(maxima, jnp.max(scores, axis=-1))
    shrink = jnp.exp(maxima - highest)
    weights = jnp.exp(scores - highest[..., None])
    totals = totals * shrink + jnp.sum(weights, axis=-1)
    weighted = weighted * shrink[..., None] + jnp.einsum(
        "tkgs,skd->tkgd",
        weights.astype(jnp.bfloat16),
        value_rows,
        preferred_element_type=jnp.float32,
    )
    return (maxima * 0.0 + highest, totals, weighted)


def per_device(queries, key_states, value_states, out_weight, noise_table, plan):
    ch_dev, tok_dev, heads_local, head_size = queries.shape
    kv_local = key_states.shape[2]
    per_kv = heads_local // kv_local
    span_count = ch_dev * lax.axis_size("span")
    first_span = lax.axis_index("span") * ch_dev
    factor = head_size ** (-0.5)
    grouped = queries.reshape(ch_dev, tok_dev, kv_local, per_kv, head_size)
    start_max = jnp.full((ch_dev, tok_dev, kv_local, per_kv), -1e30, jnp.float32)
    start_tot = jnp.zeros((ch_dev, tok_dev, kv_local, per_kv), jnp.float32)
    start_acc = jnp.zeros((ch_dev, tok_dev, kv_local, per_kv, head_size), jnp.float32)
    span_rows = (
        lax.all_gather(key_states, "seq", axis=1, tiled=True),
        lax.all_gather(value_states, "seq", axis=1, tiled=True),
    )
    key_piece = lax.all_gather(span_rows[0], "span", axis=0, tiled=True)
    value_piece = lax.all_gather(span_rows[1], "span", axis=0, tiled=True)
    new_max = []
    new_tot = []
    new_acc = []
    for q_span in range(ch_dev):
        inner_state = (start_max[q_span], start_tot[q_span], start_acc[q_span])
        for k_span in range(span_count):

            def update(inner, q_span=q_span, k_span=k_span):
                return fold_block(
                    inner, grouped[q_span], key_piece[k_span], value_piece[k_span], factor
                )

            inner_state = lax.cond(
                k_span <= first_span + q_span, update, lambda inner: inner, inner_state
            )
        new_max.append(inner_state[0])
        new_tot.append(inner_state[1])
        new_acc.append(inner_state[2])
    attn = (
        (jnp.stack(new_acc) / jnp.stack(new_tot)[..., None])
        .reshape(ch_dev, tok_dev, heads_local * head_size)
        .astype(jnp.bfloat16)
    )
    columns = jnp.einsum(
        "ctf,fo->cto",
        lax.all_gather(attn, "seq", axis=1, tiled=True),
        out_weight,
        preferred_element_type=jnp.float32,
    )
    partial_out = lax.all_to_all(
        columns.astype(jnp.bfloat16), "seq", split_axis=1, concat_axis=2, tiled=True
    ).astype(columns.dtype)
    summed = lax.psum_scatter(
        partial_out.astype(jnp.bfloat16), "tp", scatter_dimension=2, tiled=True
    ).astype(jnp.float32)
    levels = lax.dynamic_slice_in_dim(plan, first_span, ch_dev)
    picks = (levels[:, None] == jnp.arange(noise_table.shape[0], dtype=jnp.int32)[None, :]).astype(
        jnp.float32
    )
    gates = jnp.dot(picks, noise_table, precision=lax.Precision.HIGHEST)
    return (summed * gates[:, None, :]).astype(jnp.bfloat16)


def solution(mesh):
    placed = (
        P(("rep", "span"), "seq", "tp", None),
        P(("rep", "span"), "seq", "tp", None),
        P(("rep", "span"), "seq", "tp", None),
        P("tp", "seq"),
        P(None, "tp"),
        P("rep"),
    )
    return jax.shard_map(
        per_device,
        mesh=mesh,
        in_specs=placed,
        out_specs=P(("rep", "span"), "seq", "tp"),
        check_vma=False,
    )
```

profile of v0, /device:TPU:0, one launch (start us, length us, event | category | flops | bytes accessed | tf_op | source)
XLA Modules:
  0.0 320.5 jit_solution(18199733619609409647)
XLA Ops:
  6.5 1.0 copy.63
  7.5 18.0 %all_gather.15 = bf16[2,512,2,128]{3,1,2,0:T(8,128)(2,1)} all-gather(bf16[2,128,2,128]{3,1,2,0:T(8,128)(2,1)S(1)} %copy.63), channel_id=1, replica_groups=mesh['rep'=2,'span'=2,'seq'=4,'tp'=2] {'seq'}, dimensions={1}, use_global_device_ids=true | all-gather | bytes 655360 | tf_op jit(solution)/shard_map/all_gather | solution.py:38
  25.6 0.0 all-gather.6.cloned.1.call-start
  25.6 0.9 copy.64
  26.5 17.0 %all_gather.17 = bf16[2,512,2,128]{3,1,2,0:T(8,128)(2,1)} all-gather(bf16[2,128,2,128]{3,1,2,0:T(8,128)(2,1)S(1)} %copy.64), channel_id=1, replica_groups=mesh['rep'=2,'span'=2,'seq'=4,'tp'=2] {'seq'}, dimensions={1}, use_global_device_ids=true | all-gather | bytes 655360 | tf_op jit(solution)/shard_map/all_gather | solution.py:39
  43.6 0.0 all-gather.8.cloned.1.call-start
  43.7 9.6 %all-gather.6.cloned.1.call-done = bf16[4,512,2,128]{3,1,2,0:T(8,128)(2,1)} async-done(((bf16[2,512,2,128]{3,1,2,0:T(8,128)(2,1)}), bf16[4,512,2,128]{3,1,2,0:T(8,128)(2,1)}) %all-gather.6.cloned.1.call-update) | async-done | bytes 1048592 | tf_op jit(solution)/shard_map/all_gather | solution.py:42
  53.3 6.1 %conditional.12 = (f32[128,2,6]{0,2,1:T(8,128)}, f32[128,2,6]{0,2,1:T(8,128)S(1)}, f32[128,2,6,128]{3,0,2,1:T(8,128)S(1)}) conditional(s32[]{:T(128)} %convert_element_type.70, () %tuple.93, (bf16[4,512,2,128]{3,1,2,0:T(8,128)(2,1)}, bf16[2,128,2,6,128]{4,1,3,2,0:T(8,128)(2,1)}, bf16[4,512,2,128]{3,1,2,0:T(8,128)(2,1)}) %tuple.190), branch_computations={%region_16.0_spmd, %region_17.0_spmd} | conditional | flops 409147392 | bytes 11210776 | solution.py:55
  53.3 1.7 bitcast_reduce_fusion.4
  55.0 0.6 exponential_multiply_fusion.1
  55.6 1.2 fusion.85
  56.8 0.7 fusion.104
  57.5 1.9 fusion.93
  59.4 6.2 %conditional.13 = ((f32[128,2,6]{0,2,1:T(8,128)}, f32[128,2,6]{0,2,1:T(8,128)S(1)}, f32[128,2,6,128]{3,0,2,1:T(8,128)S(1)})) conditional(s32[]{:T(128)} %convert_element_type.69, (f32[128,2,6]{0,2,1:T(8,128)}, f32[128,2,6]{0,2,1:T(8,128)S(1)}, f32[128,2,6,128]{3,0,2,1:T(8,128)S(1)}) %conditional.12, (f32[128,2,6]{0,2,1:T(8,128)}, ...), branch_computations={%region_20.0_spmd, %region_21.0_spmd} | conditional | flops 409344000 | bytes 12032032 | solution.py:55
  59.4 1.7 bitcast_reduce_fusion.5
  61.1 0.7 multiply_add_fusion.5
  61.8 0.5 fusion.107
  62.3 0.7 multiply_add_fusion.4
  63.0 0.6 copy.113
  63.6 2.0 fusion.115
  65.6 6.1 %conditional.8 = (f32[128,2,6]{0,2,1:T(8,128)}, f32[128,2,6]{0,2,1:T(8,128)S(1)}, f32[128,2,6,128]{3,0,2,1:T(8,128)S(1)}) conditional(s32[]{:T(128)} %convert_element_type.66, () %tuple.87, (bf16[4,512,2,128]{3,1,2,0:T(8,128)(2,1)}, bf16[2,128,2,6,128]{4,1,3,2,0:T(8,128)(2,1)}, bf16[4,512,2,128]{3,1,2,0:T(8,128)(2,1)}) %tuple.193), branch_computations={%region_0.0_spmd, %region_1.0_spmd} | conditional | flops 409147392 | bytes 11210776 | solution.py:55
  65.6 1.7 bitcast_reduce_fusion
  67.3 0.6 exponential_multiply_fusion
  67.9 1.2 fusion.2
  69.1 0.7 fusion.21
  69.8 1.9 fusion.10
  71.8 0.2 conditional.10
  72.0 1.5 conditional.15
  72.0 0.3 copy.68
  72.2 1.2 copy.102
  73.4 1.4 conditional.11
  73.4 0.3 copy.65
  73.7 1.2 copy.100
  74.9 0.1 div.11
  75.0 1.6 copy.73
  76.6 2.9 fusion.171
  79.6 0.0 reduce-scatter.2.cloned.1.call-start
  79.6 93.0 %all-gather.8.cloned.1.call-done = bf16[2,512,1536]{2,1,0:T(8,128)(2,1)} async-done(((bf16[2,128,1536]{2,1,0:T(8,128)(2,1)}), bf16[2,512,1536]{2,1,0:T(8,128)(2,1)}) %all-gather.8.cloned.1.call-update) | async-done | bytes 3145744 | tf_op jit(solution)/shard_map/all_gather | solution.py:68
  172.6 8.1 %fusion.168 = bf16[2,512,1536]{2,1,0:T(8,128)(2,1)S(1)} fusion(bf16[2,512,1536]{2,1,0:T(8,128)(2,1)} %all-gather.8.cloned.1.call-done, bf16[1536,1536]{1,0:T(8,128)(2,1)} %param.25), kind=kOutput, calls=%fused_computation.166 | convolution fusion | flops 4833411072 | bytes 11010048 | tf_op jit(solution)/shard_map/ctf,fo->cto/dot_general | solution.py:66
  180.7 3.2 %copy.74 = bf16[2,512,1536]{2,0,1:T(2,128)(2,1)S(1)} copy(bf16[2,512,1536]{2,1,0:T(8,128)(2,1)S(1)} %fusion.168) | data formatting | bytes 6291456 | tf_op jit(solution)/shard_map/convert_element_type | solution.py:73
  183.9 73.3 %all_to_all.18 = bf16[2,512,1536]{2,0,1:T(2,128)(2,1)S(1)} all-to-all(bf16[2,512,1536]{2,0,1:T(2,128)(2,1)S(1)} %copy.74), channel_id=1, replica_groups=mesh['rep'=2,'span'=2,'seq'=4,'tp'=2] {'seq'}, dimensions={1} | all-to-all | bytes 6291456 | tf_op jit(solution)/shard_map/all_to_all | solution.py:72
  257.2 4.1 %copy.75 = bf16[2,128,4,1536]{3,2,1,0:T(4,128)(2,1)} copy(bf16[2,128,4,1536]{3,0,1,2:T(2,128)(2,1)S(1)} %bitcast.326) | data formatting | bytes 6291456 | tf_op jit(solution)/shard_map/all_to_all | solution.py:72
  261.3 6.9 %all_to_all.16 = bf16[2,128,6144]{2,1,0:T(8,128)(2,1)} reshape(bf16[2,128,4,1536]{3,2,1,0:T(4,128)(2,1)} %copy.75) | data formatting | bytes 6291456 | tf_op jit(solution)/shard_map/all_to_all | solution.py:72
  268.3 0.6 copy-done.5
  268.9 0.1 dynamic_slice.3
  269.0 0.4 fusion.172
  269.4 41.7 %reduce-scatter.2.cloned.1.call-done = bf16[2,128,3072]{2,1,0:T(8,128)(2,1)} async-done(((bf16[2,128,6144]{2,1,0:T(8,128)(2,1)}), bf16[2,128,3072]{2,1,0:T(8,128)(2,1)}) %reduce-scatter.2.cloned.1.call-update) | async-done | bytes 1572880 | tf_op jit(solution)/shard_map/reduce_scatter | solution.py:75
  311.1 2.9 multiply_convert_fusion
  (12 shorter events, 0.1 us)
Async XLA Ops:
  6.5 262.4 %copy-start = (f32[64,3072]{1,0:T(8,128)S(1)}, f32[64,3072]{1,0:T(8,128)}, u32[]{:S(2)}) copy-start(f32[64,3072]{1,0:T(8,128)} %param.26) | copy-start | bytes 2359300
  6.5 37.2 %all-gather.4.cloned.1.call-start = ((), (), s32[]{:S(2)}) async-start(), calls=%async_computation.2 | async-start | bytes 1572864 | tf_op jit(solution)/shard_map/all_gather | solution.py:41
  25.6 27.7 %all-gather.6.cloned.1.call-start = ((), (), s32[]{:S(2)}) async-start(), calls=%async_computation.3 | async-start | bytes 1572864 | tf_op jit(solution)/shard_map/all_gather | solution.py:42
  43.6 129.0 %all-gather.8.cloned.1.call-start = ((), (), s32[]{:S(2)}) async-start(), calls=%async_computation.4 | async-start | bytes 3932160 | tf_op jit(solution)/shard_map/all_gather | solution.py:68
  79.6 231.5 %reduce-scatter.2.cloned.1.call-start = ((), (), s32[]{:S(2)}) async-start(), calls=%async_computation.5 | async-start | bytes 4718592 | tf_op jit(solution)/shard_map/reduce_scatter | solution.py:75
  268.3 0.7 copy-start.5
Sparse Core Ops, SparseCore 0:
  25.7 10.8 all-gather.3
  43.7 9.5 all-gather.5
  79.7 92.8 all-gather.7
  268.4 42.6 reduce-scatter.1
where the time goes:
time: 322 us; the launch traced here: 321 us
  waiting for transfers between devices  144 us (45%)
  blocking collectives  108 us (34%)
  local copies, waits for them, and re-layouts  22.1 us (7%)
  matrix products  19.2 us (6%)
  between operations  13.2 us (4%)
  other arithmetic  12.9 us (4%)
    all_gather x1, waiting for transfers between devices, per_device(): lax.all_gather(attn, 'seq', axis=1, tiled=True)  93 us
    all_to_all x1, blocking collectives, per_device(): lax.all_to_all(columns.astype(jnp.bfloat16), 'seq', split_axis=1, concat_...  73.3 us
    reduce_scatter x1, waiting for transfers between devices, per_device(): lax.psum_scatter(partial_out.astype(jnp.bfloat16), 'tp', scatter_dimensio...  41.7 us
    all_gather x1, blocking collectives, per_device(): lax.all_gather(key_states, 'seq', axis=1, tiled=True)  18 us
    all_gather x1, blocking collectives, per_device(): lax.all_gather(value_states, 'seq', axis=1, tiled=True)  17 us
    all_to_all x2, local copies, waits for them, and re-layouts, per_device(): lax.all_to_all(columns.astype(jnp.bfloat16), 'seq', split_axis=1, concat_...  11 us
    all_gather x1, waiting for transfers between devices, per_device(): value_piece = lax.all_gather(span_rows[1], 'span', axis=0, tiled=True)  9.6 us
    dot_general x1, matrix products, per_device(): jnp.einsum('ctf,fo->cto', lax.all_gather(attn, 'seq', axis=1, tiled=True)...  8.06 us
  transfers between devices with their start and end apart: 4, of which 3 were waited for; matrix products, arithmetic and copies ran while one was open for 0% of the time, Pallas kernels for 0%

commit v1 on v0

--- a/solution.py
+++ b/solution.py
@@ -65,7 +65,7 @@
     )
     columns = jnp.einsum(
         "ctf,fo->cto",
-        lax.all_gather(attn, "seq", axis=1, tiled=True),
+        jnp.concatenate(lax.all_gather(attn, "seq"), axis=1),
         out_weight,
         preferred_element_type=jnp.float32,
     )

time: 322 us -> 320 us (level)
  no operation moved by 1% of the time
where the time goes in v1:
time: 320 us; the launch traced here: 319 us
  waiting for transfers between devices  143 us (45%)
  blocking collectives  108 us (34%)
  local copies, waits for them, and re-layouts  23.2 us (7%)
  matrix products  18.7 us (6%)
  between operations  13.2 us (4%)
  other arithmetic  11.7 us (4%)
    all_gather x1, waiting for transfers between devices, per_device(): lax.all_gather(attn, 'seq')  92 us
    all_to_all x1, blocking collectives, per_device(): lax.all_to_all(columns.astype(jnp.bfloat16), 'seq', split_axis=1, concat_...  73.3 us
    reduce_scatter x1, waiting for transfers between devices, per_device(): lax.psum_scatter(partial_out.astype(jnp.bfloat16), 'tp', scatter_dimensio...  41.7 us
    all_gather x1, blocking collectives, per_device(): lax.all_gather(key_states, 'seq', axis=1, tiled=True)  18 us
    all_gather x1, blocking collectives, per_device(): lax.all_gather(value_states, 'seq', axis=1, tiled=True)  17 us
    all_to_all x2, local copies, waits for them, and re-layouts, per_device(): lax.all_to_all(columns.astype(jnp.bfloat16), 'seq', split_axis=1, concat_...  11 us
    all_gather x1, waiting for transfers between devices, per_device(): value_piece = lax.all_gather(span_rows[1], 'span', axis=0, tiled=True)  9.6 us
    dot_general x1, matrix products, per_device(): jnp.einsum('ctf,fo->cto', jnp.concatenate(lax.all_gather(attn, 'seq'), ax...  7.58 us
  transfers between devices with their start and end apart: 4, of which 3 were waited for; matrix products, arithmetic and copies ran while one was open for 0% of the time, Pallas kernels for 0%

profile of v1, /device:TPU:0, one launch (start us, length us, event | category | flops | bytes accessed | tf_op | source)
XLA Modules:
  0.0 318.7 jit_solution(16168666967645279914)
XLA Ops:
  6.5 1.0 copy.59
  7.5 18.0 %all_gather.16 = bf16[2,512,2,128]{3,1,2,0:T(8,128)(2,1)} all-gather(bf16[2,128,2,128]{3,1,2,0:T(8,128)(2,1)S(1)} %copy.59), channel_id=1, replica_groups=mesh['rep'=2,'span'=2,'seq'=4,'tp'=2] {'seq'}, dimensions={1}, use_global_device_ids=true | all-gather | bytes 655360 | tf_op jit(solution)/shard_map/all_gather | solution.py:38
  25.6 0.0 all-gather.6.cloned.1.call-start
  25.6 0.9 copy.60
  26.5 17.0 %all_gather.18 = bf16[2,512,2,128]{3,1,2,0:T(8,128)(2,1)} all-gather(bf16[2,128,2,128]{3,1,2,0:T(8,128)(2,1)S(1)} %copy.60), channel_id=1, replica_groups=mesh['rep'=2,'span'=2,'seq'=4,'tp'=2] {'seq'}, dimensions={1}, use_global_device_ids=true | all-gather | bytes 655360 | tf_op jit(solution)/shard_map/all_gather | solution.py:39
  43.6 0.0 all-gather.6.cloned.1.call-update
  43.6 0.0 all-gather.8.cloned.1.call-start
  43.7 0.0 all-gather.4.cloned.1.call-done
  43.7 9.6 %all-gather.6.cloned.1.call-done = bf16[4,512,2,128]{3,1,2,0:T(8,128)(2,1)} async-done(((bf16[2,512,2,128]{3,1,2,0:T(8,128)(2,1)}), bf16[4,512,2,128]{3,1,2,0:T(8,128)(2,1)}) %all-gather.6.cloned.1.call-update) | async-done | bytes 1048592 | tf_op jit(solution)/shard_map/all_gather | solution.py:42
  53.3 6.1 %conditional.8 = (f32[128,2,6]{0,2,1:T(8,128)}, f32[128,2,6]{0,2,1:T(8,128)S(1)}, f32[128,2,6,128]{3,0,2,1:T(8,128)S(1)}) conditional(s32[]{:T(128)} %convert_element_type.73, () %tuple.87, (bf16[4,512,2,128]{3,1,2,0:T(8,128)(2,1)}, bf16[2,128,2,6,128]{4,1,3,2,0:T(8,128)(2,1)}, bf16[4,512,2,128]{3,1,2,0:T(8,128)(2,1)}) %tuple.180), branch_computations={%region_0.0_spmd, %region_1.0_spmd} | conditional | flops 409147392 | bytes 11210776 | solution.py:55
  53.3 1.7 bitcast_reduce_fusion
  55.0 0.6 exponential_multiply_fusion
  55.6 1.2 fusion.2
  56.8 0.7 fusion.21
  57.5 1.9 fusion.10
  59.4 6.1 %conditional.12 = (f32[128,2,6]{0,2,1:T(8,128)}, f32[128,2,6]{0,2,1:T(8,128)S(1)}, f32[128,2,6,128]{3,0,2,1:T(8,128)S(1)}) conditional(s32[]{:T(128)} %convert_element_type.77, () %tuple.93, (bf16[4,512,2,128]{3,1,2,0:T(8,128)(2,1)}, bf16[2,128,2,6,128]{4,1,3,2,0:T(8,128)(2,1)}, bf16[4,512,2,128]{3,1,2,0:T(8,128)(2,1)}) %tuple.183), branch_computations={%region_16.0_spmd, %region_17.0_spmd} | conditional | flops 409147392 | bytes 11210776 | solution.py:55
  59.4 1.7 bitcast_reduce_fusion.4
  61.1 0.6 exponential_multiply_fusion.1
  61.7 1.2 fusion.85
  62.9 0.7 fusion.104
  63.6 1.9 fusion.93
  65.5 6.2 %conditional.13 = ((f32[128,2,6]{0,2,1:T(8,128)}, f32[128,2,6]{0,2,1:T(8,128)S(1)}, f32[128,2,6,128]{3,0,2,1:T(8,128)S(1)})) conditional(s32[]{:T(128)} %convert_element_type.76, (f32[128,2,6]{0,2,1:T(8,128)}, f32[128,2,6]{0,2,1:T(8,128)S(1)}, f32[128,2,6,128]{3,0,2,1:T(8,128)S(1)}) %conditional.12, (f32[128,2,6]{0,2,1:T(8,128)}, ...), branch_computations={%region_20.0_spmd, %region_21.0_spmd} | conditional | flops 409344000 | bytes 12032032 | solution.py:55
  65.5 1.7 bitcast_reduce_fusion.5
  67.2 0.7 multiply_add_fusion.5
  67.9 0.5 fusion.107
  68.4 0.7 multiply_add_fusion.4
  69.1 2.0 fusion.115
  71.2 0.6 copy.104
  71.8 1.2 conditional.11
  71.8 1.2 copy.61
  72.9 1.2 conditional.15
  72.9 1.2 copy.64
  74.1 0.1 div.18
  74.2 1.8 fusion.171
  76.0 1.2 copy.67
  77.2 0.0 reduce-scatter.2.cloned.1.call-start
  77.2 92.0 %all-gather.8.cloned.1.call-done = bf16[4,2,128,1536]{3,2,1,0:T(8,128)(2,1)} async-done(((bf16[1,2,128,1536]{3,2,1,0:T(8,128)(2,1)}), bf16[4,2,128,1536]{3,2,1,0:T(8,128)(2,1)}) %all-gather.8.cloned.1.call-update) | async-done | bytes 3145744 | tf_op jit(solution)/shard_map/all_gather | solution.py:68
  169.2 2.1 copy.68
  171.3 7.6 %fusion.168 = bf16[2,512,1536]{2,1,0:T(8,128)(2,1)S(1)} fusion(bf16[2,512,1536]{2,1,0:T(8,128)(2,1)S(1)} %bitcast.331, bf16[1536,1536]{1,0:T(8,128)(2,1)} %param.25), kind=kOutput, calls=%fused_computation.166 | convolution fusion | flops 4833411072 | bytes 11010048 | tf_op jit(solution)/shard_map/ctf,fo->cto/dot_general | solution.py:66
  178.9 3.2 %copy.69 = bf16[2,512,1536]{2,0,1:T(2,128)(2,1)S(1)} copy(bf16[2,512,1536]{2,1,0:T(8,128)(2,1)S(1)} %fusion.168) | data formatting | bytes 6291456 | tf_op jit(solution)/shard_map/convert_element_type | solution.py:73
  182.1 73.3 %all_to_all.18 = bf16[2,512,1536]{2,0,1:T(2,128)(2,1)S(1)} all-to-all(bf16[2,512,1536]{2,0,1:T(2,128)(2,1)S(1)} %copy.69), channel_id=1, replica_groups=mesh['rep'=2,'span'=2,'seq'=4,'tp'=2] {'seq'}, dimensions={1} | all-to-all | bytes 6291456 | tf_op jit(solution)/shard_map/all_to_all | solution.py:72
  255.4 4.1 %copy.70 = bf16[2,128,4,1536]{3,2,1,0:T(4,128)(2,1)} copy(bf16[2,128,4,1536]{3,0,1,2:T(2,128)(2,1)S(1)} %bitcast.328) | data formatting | bytes 6291456 | tf_op jit(solution)/shard_map/all_to_all | solution.py:72
  259.5 6.9 %all_to_all.16 = bf16[2,128,6144]{2,1,0:T(8,128)(2,1)} reshape(bf16[2,128,4,1536]{3,2,1,0:T(4,128)(2,1)} %copy.70) | data formatting | bytes 6291456 | tf_op jit(solution)/shard_map/all_to_all | solution.py:72
  266.5 0.6 copy-done.5
  267.1 0.1 dynamic_slice.3
  267.2 0.4 fusion.172
  267.6 41.7 %reduce-scatter.2.cloned.1.call-done = bf16[2,128,3072]{2,1,0:T(8,128)(2,1)} async-done(((bf16[2,128,6144]{2,1,0:T(8,128)(2,1)}), bf16[2,128,3072]{2,1,0:T(8,128)(2,1)}) %reduce-scatter.2.cloned.1.call-update) | async-done | bytes 1572880 | tf_op jit(solution)/shard_map/reduce_scatter | solution.py:75
  309.3 2.9 multiply_convert_fusion
  (11 shorter events, 0.1 us)
Async XLA Ops:
  6.5 260.7 %copy-start = (f32[64,3072]{1,0:T(8,128)S(1)}, f32[64,3072]{1,0:T(8,128)}, u32[]{:S(2)}) copy-start(f32[64,3072]{1,0:T(8,128)} %param.26) | copy-start | bytes 2359300
  6.5 37.2 %all-gather.4.cloned.1.call-start = ((), (), s32[]{:S(2)}) async-start(), calls=%async_computation.2 | async-start | bytes 1572864 | tf_op jit(solution)/shard_map/all_gather | solution.py:41
  25.6 27.7 %all-gather.6.cloned.1.call-start = ((), (), s32[]{:S(2)}) async-start(), calls=%async_computation.3 | async-start | bytes 1572864 | tf_op jit(solution)/shard_map/all_gather | solution.py:42
  43.6 125.6 %all-gather.8.cloned.1.call-start = ((), (), s32[]{:S(2)}) async-start(), calls=%async_computation.4 | async-start | bytes 3932160 | tf_op jit(solution)/shard_map/all_gather | solution.py:68
  77.2 232.1 %reduce-scatter.2.cloned.1.call-start = ((), (), s32[]{:S(2)}) async-start(), calls=%async_computation.5 | async-start | bytes 4718592 | tf_op jit(solution)/shard_map/reduce_scatter | solution.py:75
  266.5 0.7 copy-start.5
Sparse Core Ops, SparseCore 0:
  25.7 10.8 all-gather.3
  43.7 9.5 all-gather.5
  77.3 91.8 all-gather.7
  266.6 42.6 reduce-scatter.1
